TPU v7x, 32 devices: a whole 2x2x4 slice. The times are simulated.
32 devices in a mesh: tower: 2 (over core), tp: 4 (over z), grp: 4 (over y, x).
Axes of the slice: x: 2, y: 2, z: 4, core: 2. Of those that a mesh axis runs over, the one named last changes fastest.
Arguments:
- tokens: bfloat16 [3072, 8192], P('grp', 'tp'), may hold values from -700 to 700
- modality: int32 [3072], P('grp'), may hold values from 0 to 1, as said below
- doc_ids: int32 [3072], P('grp'), may hold values from 0 to 15, as said below
- owner_ids: int32 [3072], P('grp'), may hold values from 0 to 3, as said below
- norm_gain: float32 [2, 8192], P('tower'), may hold values from 0.5 to 1.5
- query_weight: bfloat16 [2, 8192, 4096], P('tower', 'grp', 'tp'), may hold values from -0.125 to 0.125
- pair_weight: bfloat16 [2, 8192, 1024], P('tower', 'grp'), may hold values from -0.125 to 0.125
Outputs:
- attended: bfloat16 [2, 3072, 4096], P('tower', 'grp', 'tp')
Inputs may be any that keep to these rules, and one draw needn't show every extreme that they name: Every group of 768 tokens holds exactly 384 tokens of each modality. `owner_ids`: within every group each owner is named by exactly 192 tokens, and by at most 192 tokens of one modality. `doc_ids`: all tokens of one document have the same owner.
All inputs are finite; a program needn't handle non-finite values.
Results may differ from a plain program's by a relative error of at most 0.0084.
Values may be sent and summed in bfloat16 or wider, within the bound.
A program may use at most 128 MiB of HBM per device.

v0:
```python
import functools
import math

import jax
import jax.numpy as jnp
from jax import lax
from jax.experimental import pallas as pl
from jax.experimental.pallas import tpu as pltpu
from jax.sharding import PartitionSpec as P

HD = 128
EPS = 1e-05
MASKED = -1e30


def swap_tower(value):
    return lax.ppermute(value, "tower", [(0, 1), (1, 0)])


def pick(onehot, rows):
    return jnp.dot(onehot.astype(jnp.bfloat16), rows, preferred_element_type=jnp.float32).astype(
        jnp.bfloat16
    )


MESH = pl.DeviceIdType.MESH


def greet(devices):
    barrier = pltpu.get_barrier_semaphore()
    for present, device in devices:

        @pl.when(present)
        def _(device=device):
            pl.semaphore_signal(barrier, inc=1, device_id=device, device_id_type=MESH)

    pl.semaphore_wait(barrier, sum(jnp.asarray(present, jnp.int32) for present, _ in devices))


def others(axis, count):
    me = lax.axis_index(axis)
    return [(True, {axis: lax.rem(me + k, count)}) for k in range(1, count)]


def facts_kernel(groups, tp_count, facts, by_group, by_block, send_sem, group_sem, block_sem):
    group, block = lax.axis_index("grp"), lax.axis_index("tp")
    greet(others("grp", groups) + others("tp", tp_count))
    sent = []
    for k in range(1, groups):
        sent.append(
            pltpu.make_async_remote_copy(
                src_ref=facts,
                dst_ref=by_group.at[group],
                send_sem=send_sem.at[k - 1],
                recv_sem=group_sem.at[group],
                device_id={"grp": lax.rem(group + k, groups)},
                device_id_type=MESH,
            )
        )
    for k in range(1, tp_count):
        sent.append(
            pltpu.make_async_remote_copy(
                src_ref=facts,
                dst_ref=by_block.at[block],
                send_sem=send_sem.at[groups + k - 2],
                recv_sem=block_sem.at[block],
                device_id={"tp": lax.rem(block + k, tp_count)},
                device_id_type=MESH,
            )
        )
    for copy in sent:
        copy.start()
    by_group[group] = facts[...]
    by_block[block] = facts[...]
    for k in range(1, groups):
        source = lax.rem(group + k, groups)
        pltpu.make_async_copy(facts, by_group.at[source], group_sem.at[source]).wait()
    for k in range(1, tp_count):
        source = lax.rem(block + k, tp_count)
        pltpu.make_async_copy(facts, by_block.at[source], block_sem.at[source]).wait()
    for copy in sent:
        copy.wait_send()


def share_facts(facts, groups, tp_count):
    vmem = pl.BlockSpec(memory_space=pltpu.VMEM)
    return pl.pallas_call(
        functools.partial(facts_kernel, groups, tp_count),
        out_shape=[
            jax.ShapeDtypeStruct((groups,) + facts.shape, facts.dtype),
            jax.ShapeDtypeStruct((tp_count,) + facts.shape, facts.dtype),
        ],
        in_specs=[vmem],
        out_specs=[vmem, vmem],
        scratch_shapes=[
            pltpu.SemaphoreType.DMA((groups + tp_count - 2,)),
            pltpu.SemaphoreType.DMA((groups,)),
            pltpu.SemaphoreType.DMA((tp_count,)),
        ],
        compiler_params=pltpu.CompilerParams(collective_id=1, has_side_effects=True),
        name="share_facts",
    )(facts)


def tokens_kernel(
    groups, count, chunks, chosen, out, held, own_sem, line_send, line_recv, cross_send, cross_recv
):
    group, me = lax.axis_index("grp"), lax.axis_index("tp")
    rows = chosen.shape[0] // chunks
    has_left, has_right = me > 0, me < count - 1
    left, right = jnp.maximum(me - 1, 0), jnp.minimum(me + 1, count - 1)
    greet([(has_left, {"tp": left}), (has_right, {"tp": right})] + others("grp", groups))

    def part(chunk):
        return pl.ds(pl.multiple_of(chunk * rows, rows), rows)

    def hop(source, chunk, way, own):
        src = chosen if own else held.at[source]
        return pltpu.make_async_remote_copy(
            src_ref=src.at[part(chunk)],
            dst_ref=held.at[source, part(chunk)],
            send_sem=line_send.at[way, source, chunk],
            recv_sem=line_recv.at[source, chunk],
            device_id={"tp": left if way == 0 else right},
            device_id_type=MESH,
        )

    def cross(source, chunk, own):
        src = chosen if own else held.at[source]
        return pltpu.make_async_remote_copy(
            src_ref=src.at[part(chunk)],
            dst_ref=out.at[group, part(chunk)],
            send_sem=cross_send.at[source, chunk],
            recv_sem=cross_recv.at[group, chunk],
            device_id={"grp": source},
            device_id_type=MESH,
        )

    def keep(source, chunk, own):
        src = chosen if own else held.at[source]
        return pltpu.make_async_copy(
            src.at[part(chunk)], out.at[group, part(chunk)], own_sem.at[chunk]
        )

    def pass_on(source, chunk, own):
        @pl.when(source == group)
        def _():
            keep(source, chunk, own).start()

        @pl.when(source != group)
        def _():
            cross(source, chunk, own).start()

    def start_own(chunk):
        @pl.when(has_left)
        def _():
            hop(me, chunk, 0, True).start()

        @pl.when(has_right)
        def _():
            hop(me, chunk, 1, True).start()

        pass_on(me, chunk, True)

    def arrive(source, chunk, way, more):
        hop(source, chunk, way, False).wait_recv()

        @pl.when(more)
        def _():
            hop(source, chunk, way, False).start()

        pass_on(source, chunk, False)

    start_own(0)

    @pl.loop(0, chunks)
    def _(chunk):
        @pl.when(chunk + 1 < chunks)
        def _():
            start_own(chunk + 1)

        for k in range(1, count):

            @pl.when(me + k < count)
            def _():
                arrive(me + k, chunk, 0, has_left)

            @pl.when(me - k >= 0)
            def _():
                arrive(me - k, chunk, 1, has_right)

    @pl.loop(0, chunks)
    def _(chunk):
        for k in range(1, groups):
            source = lax.rem(group + k, groups)
            pltpu.make_async_copy(
                chosen.at[part(chunk)], out.at[source, part(chunk)], cross_recv.at[source, chunk]
            ).wait()
        keep(group, chunk, False).wait()
        for source in range(count):

            @pl.when(source != group)
            def _():
                cross(source, chunk, False).wait_send()

            @pl.when((source >= me) & has_left)
            def _():
                hop(source, chunk, 0, False).wait_send()

            @pl.when((source <= me) & has_right)
            def _():
                hop(source, chunk, 1, False).wait_send()


def move_tokens(chosen, groups, tp_count):
    half, width = chosen.shape
    chunks = max(1, 24 // tp_count)
    while half % chunks or (half // chunks) % 16:
        chunks -= 1
    vmem = pl.BlockSpec(memory_space=pltpu.VMEM)
    return pl.pallas_call(
        functools.partial(tokens_kernel, groups, tp_count, chunks),
        out_shape=jax.ShapeDtypeStruct((groups, half, width), chosen.dtype),
        in_specs=[vmem],
        out_specs=vmem,
        scratch_shapes=[
            pltpu.VMEM((tp_count, half, width), chosen.dtype),
            pltpu.SemaphoreType.DMA((chunks,)),
            pltpu.SemaphoreType.DMA((2, tp_count, chunks)),
            pltpu.SemaphoreType.DMA((tp_count, chunks)),
            pltpu.SemaphoreType.DMA((tp_count, chunks)),
            pltpu.SemaphoreType.DMA((groups, chunks)),
        ],
        compiler_params=pltpu.CompilerParams(
            collective_id=2, has_side_effects=True, vmem_limit_bytes=40 * 2**20
        ),
        name="move_tokens",
    )(chosen)


def to_owner(partial):
    return lax.all_to_all(partial, "grp", split_axis=0, concat_axis=0, tiled=True)


def local(tokens, modality, doc_ids, owner_ids, norm_gain, query_weight, pair_weight):
    groups = lax.axis_size("grp")
    tp_count = lax.axis_size("tp")
    tower = lax.axis_index("tower")
    group = lax.axis_index("grp")
    tp_rank = lax.axis_index("tp")
    tok, width = tokens.shape
    half = tok // 2
    slot_count = tok // groups
    head_cols = query_weight.shape[2]
    pair_heads = pair_weight.shape[2] // (2 * HD)
    own_head = tp_rank // (tp_count // pair_heads)
    features = width * tp_count
    bf16, f32, i32 = jnp.bfloat16, jnp.float32, jnp.int32

    values = tokens.astype(f32)
    code = (doc_ids * groups + owner_ids) * 2 + modality
    squares = jnp.sum(values * values, axis=1)
    row = jnp.arange(8, dtype=i32)[:, None]
    facts = jnp.where(row == 0, code.astype(f32)[None, :], jnp.where(row == 1, squares[None, :], 0.0))
    by_group, by_block = share_facts(facts, groups, tp_count)
    codes = by_group[:, 0, :].astype(i32)
    mods = codes % 2
    owners = (codes // 2) % groups
    squares = jnp.sum(by_block[:, 1, :], axis=0)
    inverse_rms = lax.rsqrt(squares / features + EPS)

    where_i = jnp.arange(tok, dtype=i32)
    before = (where_i[None, :] < where_i[:, None])[None]
    owner_rank = jnp.sum(((owners[:, None, :] == owners[:, :, None]) & before).astype(i32), axis=2)
    mod_rank = jnp.sum(((mods[:, None, :] == mods[:, :, None]) & before).astype(i32), axis=2)
    slots = owners * slot_count + owner_rank
    packed = mods * half + mod_rank
    at_slot = slots[:, None, :] == where_i[None, :, None]
    packed_of_slot = jnp.sum(jnp.where(at_slot, packed[:, None, :], 0), axis=2)

    slots_here = lax.dynamic_index_in_dim(slots, group, 0, False)
    packed_here = lax.dynamic_index_in_dim(packed, group, 0, False)

    gain = lax.dynamic_slice_in_dim(norm_gain[0], tp_rank * width, width, 0)
    normed = (values * inverse_rms[:, None] * gain[None, :]).astype(bf16)
    choose = packed_here[None, :] == (tower * half + jnp.arange(half, dtype=i32))[:, None]
    chosen = pick(choose, normed)
    arrived = move_tokens(chosen, groups, tp_count)

    pair_cut = lax.dynamic_slice_in_dim(pair_weight[0], own_head * 2 * HD, 2 * HD, 1)
    half_cols = head_cols // 2
    cols = half_cols + HD
    position = packed_of_slot - tower * half
    position = jnp.where(position < 0, position + tok, position)
    pieces = 2
    step = groups // pieces
    summed = []
    for piece in range(pieces):
        these = arrived[piece * step : (piece + 1) * step].reshape(step * half, width)
        query_part = jnp.dot(these, query_weight[0], preferred_element_type=f32).astype(bf16)
        pair_part = jnp.dot(these, pair_cut, preferred_element_type=f32).astype(bf16)

        def columns(core):
            return jnp.concatenate(
                [
                    lax.dynamic_slice_in_dim(query_part, core * half_cols, half_cols, 1),
                    lax.dynamic_slice_in_dim(pair_part, core * HD, HD, 1),
                ],
                axis=1,
            )

        got = swap_tower(columns(1 - tower))
        kept = columns(tower)
        slotted = []
        for k in range(step):
            onehot = (position[piece * step + k][:, None] == where_i[None, :]).astype(bf16)
            span = slice(k * half, (k + 1) * half)
            both = jnp.dot(onehot[:, :half], kept[span], preferred_element_type=f32)
            both += jnp.dot(onehot[:, half:], got[span], preferred_element_type=f32)
            slotted.append(both.astype(bf16).reshape(groups, slot_count, cols))
        parts = to_owner(jnp.concatenate(slotted, axis=1))
        summed.append(jnp.sum(parts.astype(f32), axis=0).astype(bf16))
    rows = jnp.concatenate(summed, axis=0)
    own_side = rows[:, half_cols:]
    far_side = swap_tower(own_side)
    keys = jnp.where(tower == 0, own_side, far_side)
    vals = jnp.where(tower == 0, far_side, own_side)

    mine = group * slot_count + jnp.arange(slot_count, dtype=i32)
    at_mine = slots[:, None, :] == mine[None, :, None]
    code_mine = jnp.sum(jnp.where(at_mine, codes[:, None, :], 0), axis=2).reshape(tok)
    place_mine = jnp.sum(jnp.where(at_mine, where_i[None, None, :], 0), axis=2)
    place_mine = (place_mine + tok * jnp.arange(groups, dtype=i32)[:, None]).reshape(tok)
    image = code_mine % 2 == 1
    doc = code_mine // (2 * groups)
    allowed = (doc[:, None] == doc[None, :]) & (
        (place_mine[None, :] <= place_mine[:, None]) | (image[:, None] & image[None, :])
    )
    heads = half_cols // HD
    queries = rows[:, :half_cols].reshape(tok, heads, HD)
    scores = jnp.einsum("qhd,kd->hqk", queries, keys, preferred_element_type=f32) * (
        1.0 / math.sqrt(HD)
    )
    scores = jnp.where(allowed[None], scores, MASKED)
    powered = jnp.exp(scores - jnp.max(scores, axis=2, keepdims=True))
    weights = (powered / jnp.sum(powered, axis=2, keepdims=True)).astype(bf16)
    mixed = jnp.einsum("hqk,kd->qhd", weights, vals, preferred_element_type=f32)
    mixed = mixed.astype(bf16).reshape(tok, half_cols)

    returned = lax.all_to_all(mixed, "grp", split_axis=0, concat_axis=0, tiled=True)
    other = swap_tower(returned)
    left = jnp.where(tower == 0, returned, other)
    right = jnp.where(tower == 0, other, returned)
    in_tower = modality == tower
    place = (slots_here[:, None] == where_i[None, :]) & in_tower[:, None]
    result = pick(place, jnp.concatenate([left, right], axis=1))
    return result[None]


def solution(mesh):
    in_specs = (
        P("grp", "tp"),
        P("grp"),
        P("grp"),
        P("grp"),
        P("tower", None),
        P("tower", "grp", "tp"),
        P("tower", "grp", None),
    )
    out_specs = P("tower", "grp", "tp")
    return jax.shard_map(local, mesh=mesh, in_specs=in_specs, out_specs=out_specs, check_vma=False)
```

profile of v0, /device:TPU:0, one launch (start us, length us, event | category | flops | bytes accessed | tf_op | source)
XLA Modules:
  0.0 262.6 jit_solution(5995156434488861590)
XLA Ops:
  0.0 2.7 %fusion.2 = f32[768]{0:T(1024)S(1)} fusion(bf16[768,2048]{1,0:T(8,128)(2,1)} %param.7), kind=kLoop, calls=%fused_computation.11 | loop fusion | flops 4717824 | bytes 3148800 | tf_op jit(solution)/shard_map/reduce_sum | solution.py:262
  2.8 0.7 select_select_fusion.facts
  3.5 10.9 %share_facts.1 = (f32[4,8,768]{2,1,0:T(8,128)}, f32[4,8,768]{2,1,0:T(8,128)}) custom-call(f32[8,768]{1,0:T(8,128)} %select_select_fusion.facts), custom_call_target="tpu_custom_call" | custom-call | tf_op jit(solution)/shard_map/share_facts/pallas_call | solution.py:87
  14.4 0.9 slice_convert_fusion
  15.3 1.0 and_select_fusion.1
  16.3 1.0 iota_compare_fusion.6
  17.4 5.2 %convert_reduce_fusion = (s32[4,768]{1,0:T(4,128)S(1)}, s32[4,768]{1,0:T(4,128)S(1)}) fusion(s32[4,768]{1,0:T(4,128)S(1)} %get-tuple-element.32, s32[4,768]{1,0:T(4,128)S(1)} %bitcast.95, pred[768,768]{1,0:T(8,128)(4,1)} %iota_compare_fusion.6, s32[4,768]{1,0:T(4,128)S(1)} %get-tuple-element.31, s32[4,768]{1,0:T(4,128)S(1)} %bitcast.96), kind=kLoop, calls=%fused_computation.5 | loop fusion | flops 18868224 | bytes 663552 | tf_op jit(solution)/shard_map/reduce_sum | solution.py:275
  22.7 1.2 select_reduce_fusion
  23.9 0.9 slice_reduce_fusion
  24.9 0.1 slice_reduce_fusion.4
  25.0 1.6 fusion.19.chosen
  26.6 109.0 %move_tokens.1 = bf16[4,384,2048]{2,1,0:T(8,128)(2,1)S(1)} custom-call(bf16[384,2048]{1,0:T(8,128)(2,1)S(1)} %fusion.19.chosen), custom_call_target="tpu_custom_call" | custom-call | tf_op jit(solution)/shard_map/move_tokens/pallas_call | solution.py:221
  135.6 2.5 fusion.108
  138.1 7.8 %fusion.30 = bf16[768,1024]{1,0:T(8,128)(2,1)} fusion(bf16[768,2048]{1,0:T(8,128)(2,1)} %bitcast.87, bf16[1,2048,1024]{2,1,0:T(8,128)(2,1)} %param.12), kind=kOutput, calls=%fused_computation.47 | convolution fusion | flops 3222011904 | bytes 8912896 | tf_op jit(solution)/shard_map/dot_general | solution.py:300
  146.0 2.9 %convolution_convert_fusion.1 = bf16[768,256]{1,0:T(8,128)(2,1)} fusion(bf16[768,2048]{1,0:T(8,128)(2,1)S(1)} %bitcast.88, bf16[1,2048,1024]{2,1,0:T(8,128)(2,1)} %param.13, s32[]{:T(128)S(6)} %select_n.162), kind=kOutput, calls=%fused_computation.56 | convolution fusion | flops 805502976 | bytes 4587524 | tf_op jit(solution)/shard_map/dot_general | solution.py:301
  148.9 1.0 constant_dynamic-slice_fusion.5
  150.0 1.5 constant_dynamic-slice_fusion.6
  151.4 0.1 pad_maximum_fusion.2
  151.5 0.1 collective-permute-start
  151.6 2.4 convolution_convert_fusion
  154.0 0.1 copy-done.8
  154.1 3.5 %fusion.33 = bf16[768,1024]{1,0:T(8,128)(2,1)S(1)} fusion(bf16[768,2048]{1,0:T(8,128)(2,1)S(1)} %bitcast.86, bf16[1,2048,1024]{2,1,0:T(8,128)(2,1)S(1)} %copy-done.8), kind=kOutput, calls=%fused_computation.48 | convolution fusion | flops 3222011904 | bytes 8912896 | tf_op jit(solution)/shard_map/dot_general | solution.py:300
  157.6 0.7 constant_dynamic-slice_fusion.1
  158.3 0.2 constant_dynamic-slice_fusion.2
  158.5 1.0 pad_maximum_fusion.3
  159.6 0.5 collective-permute-start.1
  160.0 0.4 iota_compare_fusion.4
  160.4 0.4 iota_compare_fusion.3
  160.8 0.4 iota_compare_fusion.2
  161.3 0.7 fusion.58
  162.0 0.7 fusion.55
  162.8 0.8 add_convert_fusion.3
  163.6 1.0 add_convert_fusion.2
  164.6 1.5 pad_maximum_fusion
  166.0 9.2 %all-to-all-start = ((bf16[4,384,640]{2,1,0:T(8,128)(2,1)}), bf16[4,384,640]{2,1,0:T(8,128)(2,1)S(1)}, u32[]{:S(2)}, u32[]{:S(2)}) async-start(bf16[4,384,640]{2,1,0:T(8,128)(2,1)} %pad_maximum_fusion), calls=%async_computation | async-start | bytes 3932160 | tf_op jit(solution)/shard_map/all_to_all | solution.py:242
  175.2 0.4 iota_compare_fusion.1
  175.6 1.7 fusion.52
  177.3 0.7 fusion.49
  178.1 1.9 add_convert_fusion.1
  180.0 1.9 add_convert_fusion
  181.8 1.5 pad_maximum_fusion.1
  183.3 15.6 %all-to-all-done = bf16[4,384,640]{2,1,0:T(8,128)(2,1)S(1)} async-done(((bf16[4,384,640]{2,1,0:T(8,128)(2,1)}), bf16[4,384,640]{2,1,0:T(8,128)(2,1)S(1)}, u32[]{:S(2)}, u32[]{:S(2)}) %all-to-all-start) | async-done | bytes 1966112 | tf_op jit(solution)/shard_map/all_to_all | solution.py:242
  198.9 4.4 %all-to-all-start.1 = ((bf16[4,384,640]{2,1,0:T(8,128)(2,1)}), bf16[4,384,640]{2,1,0:T(8,128)(2,1)}, u32[]{:S(2)}, u32[]{:S(2)}) async-start(bf16[4,384,640]{2,1,0:T(8,128)(2,1)} %pad_maximum_fusion.1), calls=%async_computation.1 | async-start | bytes 3932160 | tf_op jit(solution)/shard_map/all_to_all | solution.py:242
  203.3 0.7 fusion.22
  204.0 0.1 reshape.342
  204.1 0.1 broadcast_add_fusion
  204.2 0.1 add.200
  204.3 0.6 reduce_sum.107
  204.8 21.5 %all-to-all-done.1 = bf16[4,384,640]{2,1,0:T(8,128)(2,1)} async-done(((bf16[4,384,640]{2,1,0:T(8,128)(2,1)}), bf16[4,384,640]{2,1,0:T(8,128)(2,1)}, u32[]{:S(2)}, u32[]{:S(2)}) %all-to-all-start.1) | async-done | bytes 1966112 | tf_op jit(solution)/shard_map/all_to_all | solution.py:242
  226.3 2.1 reduce_sum.108
  228.4 0.1 collective-permute-start.2
  228.5 1.0 or_and_fusion
  229.5 0.1 pad_maximum_fusion.4
  229.6 0.3 copy.66
  229.8 0.2 collective-permute-done.2
  230.1 7.0 %fusion.109 = (f32[4,768]{1,0:T(4,128)S(1)}, f32[4,768,768]{1,2,0:T(8,128)}) fusion(pred[768,768]{0,1:T(8,128)(4,1)S(1)} %or_and_fusion, bf16[768,4,128]{0,2,1:T(8,128)(2,1)S(1)} %bitcast.90, bf16[768,128]{1,0:T(8,128)(2,1)S(1)} %pad_maximum_fusion.9, bf16[768,128]{1,0:T(8,128)(2,1)} %collective-permute-done.2, pred[]{:T(512)S(6)} %eq.211), kind=kOutput, calls=%fused_computation.189 | convolution fusion | flops 613516032 | bytes 11218945 | tf_op jit(solution)/shard_map/sub | solution.py:345
  237.1 4.6 %fusion.45 = bf16[768,4,128]{0,2,1:T(8,128)(2,1)S(1)} fusion(f32[4,768,768]{1,2,0:T(8,128)} %get-tuple-element.34, f32[4,768]{1,0:T(4,128)S(1)} %get-tuple-element.33, bf16[768,128]{1,0:T(8,128)(2,1)} %collective-permute-done.2, bf16[768,128]{1,0:T(8,128)(2,1)S(1)} %pad_maximum_fusion.9, pred[]{:T(512)S(6)} %eq.211), kind=kOutput, calls=%fused_computation.54 | convolution fusion | flops 609189888 | bytes 10629121 | tf_op jit(solution)/shard_map/hqk,kd->qhd/dot_general | solution.py:347
  241.7 0.6 copy.70
  242.3 0.3 all_to_all.16
  242.6 14.9 %all_to_all.22 = bf16[4,192,512]{2,1,0:T(8,128)(2,1)S(1)} all-to-all(bf16[4,192,512]{2,1,0:T(8,128)(2,1)S(1)} %all_to_all.16), channel_id=1, replica_groups=mesh['tower'=2,'tp'=4,'grp'=4] {'grp'}, dimensions={0} | all-to-all | bytes 1572864 | tf_op jit(solution)/shard_map/all_to_all | solution.py:350
  257.6 0.1 collective-permute-start.3
  257.7 2.2 collective-permute-done.3
  259.8 0.2 broadcast_select_fusion.1
  260.0 2.6 fusion.39
  (42 shorter events, 0.3 us)
Async XLA Ops:
  0.0 24.9 %copy-start = (f32[1,8192]{1,0:T(1,128)S(1)}, f32[1,8192]{1,0:T(1,128)}, u32[]{:S(2)}) copy-start(f32[1,8192]{1,0:T(1,128)} %param.11) | copy-start | bytes 98308
  0.0 2.8 %copy-start.6 = (s32[768]{0:T(1024)S(1)}, s32[768]{0:T(1024)}, u32[]{:S(2)}) copy-start(s32[768]{0:T(1024)} %param.10) | copy-start | bytes 9220
  0.0 2.8 %copy-start.5 = (s32[768]{0:T(1024)S(1)}, s32[768]{0:T(1024)}, u32[]{:S(2)}) copy-start(s32[768]{0:T(1024)} %param.8) | copy-start | bytes 9220
  0.0 2.8 %copy-start.7 = (s32[768]{0:T(1024)S(1)}, s32[768]{0:T(1024)}, u32[]{:S(2)}) copy-start(s32[768]{0:T(1024)} %param.9) | copy-start | bytes 9220
  0.0 24.9 %copy-start.2 = (bf16[768,2048]{1,0:T(8,128)(2,1)S(1)}, bf16[768,2048]{1,0:T(8,128)(2,1)}, u32[]{:S(2)}) copy-start(bf16[768,2048]{1,0:T(8,128)(2,1)} %param.7) | copy-start | bytes 9437188
  138.1 7.8 %copy-start.3 = (bf16[2,384,2048]{2,1,0:T(8,128)(2,1)S(1)}, bf16[2,384,2048]{2,1,0:T(8,128)(2,1)}, u32[]{:S(2)}) copy-start(bf16[2,384,2048]{2,1,0:T(8,128)(2,1)} %get-tuple-element.19) | copy-start | bytes 9437188
  151.5 11.2 %collective-permute-start = (bf16[768,640]{1,0:T(8,128)(2,1)S(1)}, bf16[768,640]{1,0:T(8,128)(2,1)S(1)}, u32[]{:S(2)}, u32[]{:S(2)}) collective-permute-start(bf16[768,640]{1,0:T(8,128)(2,1)S(1)} %pad_maximum_fusion.2), channel_id=1, source_target_pairs={{0,16},{16,0},{1,17},{17,1},{2,18},{18,2},{3,19},{19,3},{4,20},{20... | collective-permute-start | bytes 2949128 | tf_op jit(solution)/shard_map/ppermute | solution.py:17
  151.6 2.5 copy-start.8
  159.6 18.5 %collective-permute-start.1 = (bf16[768,640]{1,0:T(8,128)(2,1)}, bf16[768,640]{1,0:T(8,128)(2,1)}, u32[]{:S(2)}, u32[]{:S(2)}) collective-permute-start(bf16[768,640]{1,0:T(8,128)(2,1)} %pad_maximum_fusion.3), channel_id=1, source_target_pairs={{0,16},{16,0},{1,17},{17,1},{2,18},{18,2},{3,19},{19,3},{4,20},{20... | collective-permute-start | bytes 2949128 | tf_op jit(solution)/shard_map/ppermute | solution.py:17
  166.0 32.8 %all-to-all-start = ((bf16[4,384,640]{2,1,0:T(8,128)(2,1)}), bf16[4,384,640]{2,1,0:T(8,128)(2,1)S(1)}, u32[]{:S(2)}, u32[]{:S(2)}) async-start(bf16[4,384,640]{2,1,0:T(8,128)(2,1)} %pad_maximum_fusion), calls=%async_computation | async-start | bytes 3932160 | tf_op jit(solution)/shard_map/all_to_all | solution.py:242
  175.2 2.1 copy-start.4
  198.9 27.5 %all-to-all-start.1 = ((bf16[4,384,640]{2,1,0:T(8,128)(2,1)}), bf16[4,384,640]{2,1,0:T(8,128)(2,1)}, u32[]{:S(2)}, u32[]{:S(2)}) async-start(bf16[4,384,640]{2,1,0:T(8,128)(2,1)} %pad_maximum_fusion.1), calls=%async_computation.1 | async-start | bytes 3932160 | tf_op jit(solution)/shard_map/all_to_all | solution.py:242
  228.4 1.6 collective-permute-start.2
  257.6 2.3 collective-permute-start.3
  260.0 2.6 copy-start.1
where the time goes:
time: 263 us
  Pallas kernels  120 us (46%)
  matrix products  41.9 us (16%)
  waiting for transfers between devices  39.5 us (15%)
  other arithmetic  24.1 us (9%)
  blocking collectives  14.9 us (6%)
  starting transfers between devices  14.3 us (5%)
  local copies, waits for them, and re-layouts  7.49 us (3%)
    pallas_call x1, Pallas kernels, move_tokens(): pl.pallas_call(functools.partial(tokens_kernel, groups, tp_count, chunks)...  109 us
    all_to_all x2, waiting for transfers between devices, to_owner(): lax.all_to_all(partial, 'grp', split_axis=0, concat_axis=0, tiled=True)  37.1 us
    all_to_all x1, blocking collectives, local(): lax.all_to_all(mixed, 'grp', split_axis=0, concat_axis=0, tiled=True)  14.9 us
    all_to_all x2, starting transfers between devices, to_owner(): lax.all_to_all(partial, 'grp', split_axis=0, concat_axis=0, tiled=True)  13.6 us
    dot_general x2, matrix products, local(): jnp.dot(these, query_weight[0], preferred_element_type=f32).astype(bf16)  11.3 us
    pallas_call x1, Pallas kernels, share_facts(): pl.pallas_call(functools.partial(facts_kernel, groups, tp_count), out_sha...  10.9 us
    sub x1, matrix products, local(): powered = jnp.exp(scores - jnp.max(scores, axis=2, keepdims=True))  6.99 us
    dot_general x4, matrix products, local(): both += jnp.dot(onehot[:, half:], got[span], preferred_element_type=f32)  5.53 us
  transfers between devices with their start and end apart: 6, of which 4 were waited for; matrix products, arithmetic and copies ran while one was open for 9% of the time, Pallas kernels for 0%

commit v1 on v0

v1 whole, which is shorter than its diff:
```python
import functools
import math

import jax
import jax.numpy as jnp
from jax import lax
from jax.experimental import pallas as pl
from jax.experimental.pallas import tpu as pltpu
from jax.sharding import PartitionSpec as P

HD = 128
EPS = 1e-05
MASKED = -1e30
RUN = 16
MESH = pl.DeviceIdType.MESH
BF16, F32, I32 = jnp.bfloat16, jnp.float32, jnp.int32


def dot(a, b, contract):
    return lax.dot_general(a, b, (contract, ((), ())), preferred_element_type=F32)


def iota(shape, axis):
    return lax.broadcasted_iota(I32, shape, axis)


def joint_kernel(
    sizes,
    facts,
    tokens_hbm,
    gain_hbm,
    query_hbm,
    pair_hbm,
    ret,
    place,
    tokens,
    gain,
    weight,
    onehot,
    squares,
    squares_all,
    codes,
    codes_all,
    columns,
    chosen,
    held,
    arrived,
    normed,
    own,
    swap_out,
    swap_in,
    land,
    rows,
    kv,
    mixed,
    load_sem,
    sq_send,
    sq_recv,
    code_send,
    code_recv,
    line_send,
    line_recv,
    cross_send,
    cross_recv,
    keep_sem,
    share_send,
    share_recv,
    swap_send,
    swap_recv,
    part_send,
    part_recv,
    kv_send,
    kv_recv,
    ret_send,
    ret_recv,
    both_send,
    both_recv,
):
    groups, count, chunks, pair_heads, block = sizes
    tower, me, group = lax.axis_index("tower"), lax.axis_index("tp"), lax.axis_index("grp")
    other = 1 - tower
    tok, half = tokens.shape
    half_cols = weight.shape[2] - HD
    span = groups * RUN
    heads = half_cols // HD
    width = 2 * half
    has_left, has_right = me > 0, me < count - 1
    left, right = jnp.maximum(me - 1, 0), jnp.minimum(me + 1, count - 1)
    mine = pl.ds(pl.multiple_of(tower * half, half), half)

    barrier = pltpu.get_barrier_semaphore()
    greeted = [{"grp": lax.rem(group + k, groups)} for k in range(1, groups)]
    index = tower * count + me
    line = []
    for k in range(1, 2 * count):
        there = lax.rem(index + k, 2 * count)
        line.append((there, {"tower": there // count, "tp": lax.rem(there, count)}))
    greeted += [device for _, device in line]
    for device in greeted:
        pl.semaphore_signal(barrier, inc=1, device_id=device, device_id_type=MESH)

    token_load = pltpu.make_async_copy(tokens_hbm.at[:, mine], tokens, load_sem.at[0])
    token_load.start()
    gain_load = pltpu.make_async_copy(
        gain_hbm.at[:, pl.ds(pl.multiple_of(group * width, width), width)], gain, load_sem.at[1]
    )
    gain_load.start()
    loads = [gain_load]
    own_head = me // (count // pair_heads)
    for side in range(2):
        loads.append(
            pltpu.make_async_copy(
                query_hbm.at[:, pl.ds(side * half_cols, half_cols)],
                weight.at[side, :, pl.ds(0, half_cols)],
                load_sem.at[2 + side],
            )
        )
        loads.append(
            pltpu.make_async_copy(
                pair_hbm.at[:, pl.ds(pl.multiple_of(own_head * 2 * HD + side * HD, HD), HD)],
                weight.at[side, :, pl.ds(half_cols, HD)],
                load_sem.at[4 + side],
            )
        )
    for load in loads[1:]:
        load.start()

    owner = facts[0:1, :]
    owner_of = (iota((groups, tok), 0).astype(F32) == owner).astype(F32)
    earlier = (iota((tok, tok), 0) < iota((tok, tok), 1)).astype(F32).astype(BF16)
    ranks = dot(owner_of.astype(BF16), earlier, ((1,), (0,)))
    rank = jnp.sum(owner_of * ranks, axis=0, keepdims=True).astype(I32)
    chunk_of = lax.shift_right_logical(rank, int(math.log2(RUN)))
    spot = chunk_of * span + owner.astype(I32) * RUN + (rank - chunk_of * RUN)
    place[...] = jnp.broadcast_to(spot, place.shape)
    onehot[...] = (iota((tok, tok), 0) == spot).astype(F32).astype(BF16)

    token_load.wait()

    def choose(chunk):
        piece = onehot[pl.ds(pl.multiple_of(chunk * span, span), span), :]
        picked = dot(piece, tokens[...], ((1,), (0,))).astype(BF16)
        chosen[chunk] = picked.reshape(groups, RUN, half)

    ahead = min(3, chunks)
    for chunk in range(ahead):
        choose(chunk)

    values = tokens[...].astype(F32)
    exact = values * values
    high = exact.astype(BF16)
    low = (exact - high.astype(F32)).astype(BF16)
    ones = jnp.ones((8, half), BF16)
    squares[...] = dot(ones, high, ((1,), (1,))) + dot(ones, low, ((1,), (1,)))
    squares_all[index] = squares[...]

    pl.semaphore_wait(barrier, len(greeted))

    sq_copies = [
        pltpu.make_async_remote_copy(
            src_ref=squares,
            dst_ref=squares_all.at[index],
            send_sem=sq_send.at[k],
            recv_sem=sq_recv.at[index],
            device_id=device,
            device_id_type=MESH,
        )
        for k, (_, device) in enumerate(line)
    ]

    def hop(source, chunk, way, mine_own):
        src = chosen if mine_own else held.at[source]
        return pltpu.make_async_remote_copy(
            src_ref=src.at[chunk],
            dst_ref=held.at[source, chunk],
            send_sem=line_send.at[way, source, chunk],
            recv_sem=line_recv.at[source, chunk],
            device_id={"tp": left if way == 0 else right},
            device_id_type=MESH,
        )

    def cross(source, chunk, mine_own):
        src = chosen if mine_own else held.at[source]
        return pltpu.make_async_remote_copy(
            src_ref=src.at[chunk],
            dst_ref=arrived.at[chunk, :, group, :, mine],
            send_sem=cross_send.at[source, chunk],
            recv_sem=cross_recv.at[group, chunk],
            device_id={"grp": source},
            device_id_type=MESH,
        )

    def keep(source, chunk, mine_own):
        src = chosen if mine_own else held.at[source]
        return pltpu.make_async_copy(
            src.at[chunk], arrived.at[chunk, :, group, :, mine], keep_sem.at[chunk]
        )

    def pass_on(source, chunk, mine_own):
        @pl.when(source == group)
        def _():
            keep(source, chunk, mine_own).start()

        @pl.when(source != group)
        def _():
            cross(source, chunk, mine_own).start()

    def start_own(chunk):
        @pl.when(has_left)
        def _():
            hop(me, chunk, 0, True).start()

        @pl.when(has_right)
        def _():
            hop(me, chunk, 1, True).start()

        pass_on(me, chunk, True)

    def arrive(source, chunk, way, more):
        hop(source, chunk, way, False).wait_recv()

        @pl.when(more)
        def _():
            hop(source, chunk, way, False).start()

        pass_on(source, chunk, False)

    def arrivals(chunk, k):
        @pl.when(me + k < count)
        def _():
            arrive(me + k, chunk, 0, has_left)

        @pl.when(me - k >= 0)
        def _():
            arrive(me - k, chunk, 1, has_right)

    def share(chunk):
        return pltpu.make_async_remote_copy(
            src_ref=arrived.at[chunk, :, :, :, mine],
            dst_ref=arrived.at[chunk, :, :, :, mine],
            send_sem=share_send.at[chunk],
            recv_sem=share_recv.at[chunk],
            device_id={"tower": other},
            device_id_type=MESH,
        )

    def gathered(chunk):
        for k in range(1, groups):
            source = lax.rem(group + k, groups)
            pltpu.make_async_copy(
                chosen.at[chunk], arrived.at[chunk, :, source, :, mine], cross_recv.at[source, chunk]
            ).wait()
        keep(group, chunk, False).wait()
        share(chunk).start()

    def swap(chunk):
        return pltpu.make_async_remote_copy(
            src_ref=swap_out.at[chunk],
            dst_ref=swap_in.at[chunk],
            send_sem=swap_send.at[chunk],
            recv_sem=swap_recv.at[chunk],
            device_id={"tower": other},
            device_id_type=MESH,
        )

    def project(chunk):
        share(chunk).wait_recv()

        @pl.loop(0, groups)
        def _(o):
            scale = columns[chunk, o].reshape(span, 8)[:, 0:1]
            x = arrived[chunk, o].reshape(span, width).astype(F32)
            normed[pl.ds(pl.multiple_of(o * span, span), span), :] = (x * scale * gain[...]).astype(BF16)

        sent = dot(normed[...], weight[other], ((1,), (0,)))
        swap_out[chunk] = sent.astype(BF16).reshape(groups, span, half_cols + HD)
        kept = dot(normed[...], weight[tower], ((1,), (0,)))
        own[...] = kept.reshape(groups, span, half_cols + HD)
        swap(chunk).start()

    def part(o, chunk):
        return pltpu.make_async_remote_copy(
            src_ref=swap_out.at[chunk, o],
            dst_ref=land.at[group, chunk],
            send_sem=part_send.at[o, chunk],
            recv_sem=part_recv.at[group, chunk],
            device_id={"grp": o},
            device_id_type=MESH,
        )

    def combine(chunk):
        swap(chunk).wait()

        @pl.loop(0, groups)
        def _(o):
            kind = columns[chunk, o].reshape(span, 8)[:, 1:2]
            got = swap_in[chunk, o].astype(F32)
            swap_out[chunk, o] = jnp.where(kind == tower.astype(F32), own[o], got).astype(BF16)

        for k in range(1, groups):
            part(lax.rem(group + k, groups), chunk).start()
        land[group, chunk] = swap_out[chunk, group]

    def give_kv(chunk):
        return pltpu.make_async_remote_copy(
            src_ref=kv.at[tower, chunk],
            dst_ref=kv.at[tower, chunk],
            send_sem=kv_send.at[chunk],
            recv_sem=kv_recv.at[chunk],
            device_id={"tower": other},
            device_id_type=MESH,
        )

    def total(chunk):
        for k in range(1, groups):
            source = lax.rem(group + k, groups)
            pltpu.make_async_copy(
                swap_out.at[chunk, source], land.at[source, chunk], part_recv.at[source, chunk]
            ).wait()
        summed = land[0, chunk].astype(F32)
        for source in range(1, groups):
            summed += land[source, chunk].astype(F32)
        summed = summed.astype(BF16)
        rows[chunk] = summed[:, :half_cols]
        kv[tower, chunk] = summed[:, half_cols:]
        give_kv(chunk).start()

    for chunk in range(min(ahead, 2)):
        start_own(chunk)
    for copy in sq_copies:
        copy.start()

    for there, _ in line:
        pltpu.make_async_copy(squares, squares_all.at[there], sq_recv.at[there]).wait()
    sum_squares = squares_all[0][0:1, :]
    for k in range(1, 2 * count):
        sum_squares += squares_all[k][0:1, :]
    inverse = lax.rsqrt(sum_squares / (width * count) + EPS)
    inverse_high = inverse.astype(BF16).astype(F32)
    rest = inverse - inverse_high
    inverse_mid = rest.astype(BF16).astype(F32)
    inverse_low = rest - inverse_mid
    position = iota((1, tok), 1)
    position_high = lax.shift_right_logical(position, 5)
    position_low = position - position_high * 32
    row = iota((16, tok), 0)
    stack = jnp.zeros((16, tok), F32)
    for k, line_values in enumerate(
        (
            inverse_high,
            inverse_mid,
            inverse_low,
            facts[1:2, :],
            facts[2:3, :],
            position_high.astype(F32),
            position_low.astype(F32),
        )
    ):
        stack = jnp.where(row == k, line_values, stack)
    ordered = dot(stack.astype(BF16), onehot[...], ((1,), (1,)))
    row = iota((8, tok), 0)
    packed = jnp.where(row == 0, ordered[0:1] + ordered[1:2] + ordered[2:3], 0.0)
    packed = jnp.where(row == 1, ordered[3:4], packed)
    packed = jnp.where(row == 2, ordered[4:5], packed)
    global_position = ordered[5:6] * 32.0 + ordered[6:7] + (group * tok).astype(F32)
    packed = jnp.where(row == 3, global_position, packed)
    codes[...] = packed
    codes_all[group] = packed

    def code_copy(k):
        return pltpu.make_async_remote_copy(
            src_ref=codes,
            dst_ref=codes_all.at[group],
            send_sem=code_send.at[k - 1],
            recv_sem=code_recv.at[group],
            device_id={"grp": lax.rem(group + k, groups)},
            device_id_type=MESH,
        )

    for k in range(1, groups):
        code_copy(k).start()

    def finish_codes():
        for load in loads:
            load.wait()
        for k in range(1, groups):
            source = lax.rem(group + k, groups)
            pltpu.make_async_copy(codes, codes_all.at[source], code_recv.at[source]).wait()
        for g in range(groups):
            columns[:, :, g] = jnp.transpose(codes_all[g]).reshape(chunks, groups, RUN, 8)

    def step(chunk):
        @pl.when(chunk + 2 < chunks)
        def _():
            start_own(chunk + 2)

        @pl.when(chunk + ahead < chunks)
        def _():
            choose(chunk + ahead)

        def stage_gather():
            @pl.when((chunk >= 1) & (chunk <= chunks))
            def _():
                gathered(chunk - 1)

        def stage_project():
            @pl.when((chunk >= 1) & (chunk <= chunks))
            def _():
                project(chunk - 1)

        for k in range(1, count):

            @pl.when(chunk < chunks)
            def _():
                arrivals(chunk, k)

            if k == 1:
                stage_gather()
            if k == min(2, count - 1):
                stage_project()

        @pl.when(chunk == 0)
        def _():
            finish_codes()

        @pl.when((chunk >= 1) & (chunk <= chunks))
        def _():
            combine(chunk - 1)

        @pl.when(chunk >= 2)
        def _():
            total(chunk - 2)

    @pl.loop(0, chunks + 2)
    def _(chunk):
        step(chunk)

    @pl.loop(0, chunks)
    def _(chunk):
        give_kv(chunk).wait_recv()

    total_rows = chunks * span
    facts_row = jnp.transpose(columns[:, group].reshape(total_rows, 8))
    kind_k, doc_k, place_k = facts_row[1:2], facts_row[2:3], facts_row[3:4]

    def back(target, part_block, to_grp):
        chunk = pl.ds(part_block * block, block)
        return pltpu.make_async_remote_copy(
            src_ref=mixed.at[chunk, target],
            dst_ref=ret.at[chunk, group, :, pl.ds(pl.multiple_of(tower * half_cols, half_cols), half_cols)],
            send_sem=ret_send.at[target, part_block],
            recv_sem=ret_recv.at[group, part_block],
            device_id={"grp": to_grp},
            device_id_type=MESH,
        )

    def back_local(part_block):
        chunk = pl.ds(part_block * block, block)
        return pltpu.make_async_copy(
            mixed.at[chunk, group],
            ret.at[chunk, group, :, pl.ds(pl.multiple_of(tower * half_cols, half_cols), half_cols)],
            ret_recv.at[group, part_block],
        )

    def both(source, part_block):
        chunk = pl.ds(part_block * block, block)
        where = ret.at[chunk, source, :, pl.ds(pl.multiple_of(tower * half_cols, half_cols), half_cols)]
        return pltpu.make_async_remote_copy(
            src_ref=where,
            dst_ref=where,
            send_sem=both_send.at[source, part_block],
            recv_sem=both_recv.at[source, part_block],
            device_id={"tower": other},
            device_id_type=MESH,
        )

    keys = kv.at[0]
    vals = kv.at[1]

    def attend(chunk):
        query = jnp.concatenate([rows[chunk, :, h * HD : (h + 1) * HD] for h in range(heads)], axis=0)
        column = columns[chunk, group].reshape(span, 8)
        kind_q, doc_q, place_q = column[:, 1:2], column[:, 2:3], column[:, 3:4]
        same = doc_q == doc_k
        seen = (place_k <= place_q) | ((kind_q + kind_k) == 2.0)
        bias = jnp.where(same & seen, 0.0, MASKED)
        scores = dot(query, keys[...].reshape(total_rows, HD), ((1,), (1,)))
        scores = scores * (1.0 / math.sqrt(HD)) + jnp.concatenate([bias] * heads, axis=0)
        powered = jnp.exp(scores - jnp.max(scores, axis=1, keepdims=True))
        weights = (powered / jnp.sum(powered, axis=1, keepdims=True)).astype(BF16)
        out = dot(weights, vals[...].reshape(total_rows, HD), ((1,), (0,))).astype(BF16)
        for h in range(heads):
            mixed[chunk, :, :, h * HD : (h + 1) * HD] = out[h * span : (h + 1) * span].reshape(groups, RUN, HD)

    blocks = chunks // block

    @pl.loop(0, blocks)
    def _(part_block):
        @pl.loop(0, block)
        def _(inner):
            attend(part_block * block + inner)

        for k in range(1, groups):
            target = lax.rem(group + k, groups)
            back(target, part_block, target).start()
        back_local(part_block).start()

    @pl.loop(0, blocks)
    def _(part_block):
        for k in range(1, groups):
            source = lax.rem(group + k, groups)
            pltpu.make_async_copy(
                mixed.at[pl.ds(part_block * block, block), source],
                ret.at[
                    pl.ds(part_block * block, block),
                    source,
                    :,
                    pl.ds(pl.multiple_of(tower * half_cols, half_cols), half_cols),
                ],
                ret_recv.at[source, part_block],
            ).wait()
            both(source, part_block).start()
        back_local(part_block).wait()
        both(group, part_block).start()

    for copy in sq_copies:
        copy.wait_send()
    for k in range(1, groups):
        code_copy(k).wait_send()

    @pl.loop(0, chunks)
    def _(chunk):
        for source in range(count):

            @pl.when(source != group)
            def _():
                cross(source, chunk, False).wait_send()

            @pl.when((source >= me) & has_left)
            def _():
                hop(source, chunk, 0, False).wait_send()

            @pl.when((source <= me) & has_right)
            def _():
                hop(source, chunk, 1, False).wait_send()

        share(chunk).wait_send()
        give_kv(chunk).wait_send()
        for k in range(1, groups):
            part(lax.rem(group + k, groups), chunk).wait_send()

    @pl.loop(0, blocks)
    def _(part_block):
        for k in range(1, groups):
            target = lax.rem(group + k, groups)
            back(target, part_block, target).wait_send()
        for source in range(groups):
            both(source, part_block).wait_recv()
            both(source, part_block).wait_send()


def joint(facts, tokens, gain, query_weight, pair_weight, groups, count, heads_total):
    tok, width = tokens.shape
    half = width // 2
    head_cols = query_weight.shape[1]
    half_cols = head_cols // 2
    cols = half_cols + HD
    slots = tok // groups
    chunks = slots // RUN
    span = groups * RUN
    block = chunks // 4 if chunks % 4 == 0 else 1
    blocks = chunks // block
    vmem = pl.BlockSpec(memory_space=pltpu.VMEM)
    hbm = pl.BlockSpec(memory_space=pl.ANY)
    dma = pltpu.SemaphoreType.DMA
    return pl.pallas_call(
        functools.partial(joint_kernel, (groups, count, chunks, heads_total, block)),
        out_shape=[
            jax.ShapeDtypeStruct((chunks, groups, RUN, head_cols), BF16),
            jax.ShapeDtypeStruct((8, tok), I32),
        ],
        in_specs=[vmem, hbm, hbm, hbm, hbm],
        out_specs=[vmem, vmem],
        scratch_shapes=[
            pltpu.VMEM((tok, half), BF16),
            pltpu.VMEM((1, width), F32),
            pltpu.VMEM((2, width, cols), BF16),
            pltpu.VMEM((tok, tok), BF16),
            pltpu.VMEM((8, tok), F32),
            pltpu.VMEM((2 * count, 8, tok), F32),
            pltpu.VMEM((8, tok), F32),
            pltpu.VMEM((groups, 8, tok), F32),
            pltpu.VMEM((chunks, groups, groups, RUN, 8), F32),
            pltpu.VMEM((chunks, groups, RUN, half), BF16),
            pltpu.VMEM((count, chunks, groups, RUN, half), BF16),
            pltpu.VMEM((chunks, groups, groups, RUN, width), BF16),
            pltpu.VMEM((groups * span, width), BF16),
            pltpu.VMEM((groups, span, cols), F32),
            pltpu.VMEM((chunks, groups, span, cols), BF16),
            pltpu.VMEM((chunks, groups, span, cols), BF16),
            pltpu.VMEM((groups, chunks, span, cols), BF16),
            pltpu.VMEM((chunks, span, half_cols), BF16),
            pltpu.VMEM((2, chunks, span, HD), BF16),
            pltpu.VMEM((chunks, groups, RUN, half_cols), BF16),
            dma((6,)),
            dma((2 * count,)),
            dma((2 * count,)),
            dma((groups,)),
            dma((groups,)),
            dma((2, count, chunks)),
            dma((count, chunks)),
            dma((count, chunks)),
            dma((groups, chunks)),
            dma((chunks,)),
            dma((chunks,)),
            dma((chunks,)),
            dma((chunks,)),
            dma((chunks,)),
            dma((groups, chunks)),
            dma((groups, chunks)),
            dma((chunks,)),
            dma((chunks,)),
            dma((groups, blocks)),
            dma((groups, blocks)),
            dma((groups, blocks)),
            dma((groups, blocks)),
        ],
        compiler_params=pltpu.CompilerParams(
            collective_id=1, has_side_effects=True, vmem_limit_bytes=63 * 2**20
        ),
        name="joint",
    )(facts, tokens, gain, query_weight, pair_weight)


def local(tokens, modality, doc_ids, owner_ids, norm_gain, query_weight, pair_weight):
    groups = lax.axis_size("grp")
    count = lax.axis_size("tp")
    tower = lax.axis_index("tower")
    tok = tokens.shape[0]
    head_cols = query_weight.shape[2]
    pair_heads = pair_weight.shape[2] // (2 * HD)
    row = jnp.arange(8, dtype=I32)[:, None]
    facts = jnp.where(
        row == 0, owner_ids[None], jnp.where(row == 1, modality[None], jnp.where(row == 2, doc_ids[None], 0))
    ).astype(F32)
    ret, place = joint(
        facts, tokens, norm_gain, query_weight[0], pair_weight[0], groups, count, pair_heads
    )
    ret = ret.reshape(tok, head_cols)
    chosen = (place[0][:, None] == jnp.arange(tok, dtype=I32)[None, :]) & (modality == tower)[:, None]
    result = jnp.dot(chosen.astype(BF16), ret, preferred_element_type=F32).astype(BF16)
    return result[None]


def solution(mesh):
    in_specs = (
        P("grp", "tp"),
        P("grp"),
        P("grp"),
        P("grp"),
        P("tower", None),
        P("tower", "grp", "tp"),
        P("tower", "grp", None),
    )
    out_specs = P("tower", "grp", "tp")
    return jax.shard_map(local, mesh=mesh, in_specs=in_specs, out_specs=out_specs, check_vma=False)
```

time: 263 us -> 197 us (0.75)
  Pallas kernels: 120 us -> 190 us
  waiting for transfers between devices: 39.5 us -> 0 us
  matrix products: 41.9 us -> 3.98 us
  other arithmetic: 24.1 us -> 2.11 us
  blocking collectives: 14.9 us -> 0 us
  starting transfers between devices: 14.3 us -> 0 us
  local copies, waits for them, and re-layouts: 7.49 us -> 0.75 us
    pallas_call x2 -> x1, Pallas kernels: 120 us -> 190 us  [joint(): pl.pallas_call(functools.partial(joint_kernel, (groups, count, chunks, he...]
    all_to_all x2 -> x0, waiting for transfers between devices: 37.1 us -> none  [to_owner(): lax.all_to_all(partial, 'grp', split_axis=0, concat_axis=0, tiled=True)]
    dot_general x15 -> x1, matrix products: 34.9 us -> 3.98 us  [local(): jnp.dot(chosen.astype(BF16), ret, preferred_element_type=F32).astype(BF16)]
    all_to_all x1 -> x0, blocking collectives: 14.9 us -> none  [local(): lax.all_to_all(mixed, 'grp', split_axis=0, concat_axis=0, tiled=True)]
    all_to_all x2 -> x0, starting transfers between devices: 13.6 us -> none  [to_owner(): lax.all_to_all(partial, 'grp', split_axis=0, concat_axis=0, tiled=True)]
    reduce_sum x7 -> x0, other arithmetic: 13.4 us -> none  [the longest x1 5.23 us: local(): jnp.sum(((mods[:, None, :] == mods[:, :, None]) & before).astype(i32), ax...]
    sub x1 -> x0, matrix products: 6.99 us -> none  [local(): powered = jnp.exp(scores - jnp.max(scores, axis=2, keepdims=True))]
    concatenate x5 -> x0, other arithmetic: 4.07 us -> none  [the longest x2 2.9 us: local(): parts = to_owner(jnp.concatenate(slotted, axis=1))]
  transfers between devices with their start and end apart: 6 -> 0, of which waited for: 4 -> 0; matrix products, arithmetic and copies ran while one was open for 9% -> 0% of each run, Pallas kernels for 0% -> 0%
where the time goes in v1:
time: 197 us
  Pallas kernels  190 us (96%)
  matrix products  3.98 us (2%)
  other arithmetic  2.11 us (1%)
    pallas_call x1, Pallas kernels, joint(): pl.pallas_call(functools.partial(joint_kernel, (groups, count, chunks, he...  190 us
    dot_general x1, matrix products, local(): jnp.dot(chosen.astype(BF16), ret, preferred_element_type=F32).astype(BF16)  3.98 us

profile of v1, /device:TPU:0, one launch (start us, length us, event | category | flops | bytes accessed | tf_op | source)
XLA Modules:
  0.0 196.6 jit_solution(10353397591766872128)
XLA Ops:
  0.0 0.7 broadcast_compare_fusion
  0.7 1.4 select_convert_fusion.facts
  2.1 189.7 %joint.1 = (bf16[12,4,16,1024]{3,2,1,0:T(8,128)(2,1)}, s32[8,768]{1,0:T(8,128)}) custom-call(f32[8,768]{1,0:T(8,128)} %select_convert_fusion.facts, bf16[768,2048]{1,0:T(8,128)(2,1)} %tokens_hbm.1, f32[1,8192]{1,0:T(1,128)} %gain_hbm.1, bf16[2048,1024]{1,0:T(8,128)(2,1)} %bitcast.6, bf16[2048,1024]{1,0:T(8,128)(2,1)} %bitcast.7), custom_call_target="tpu_custom_call" | custom-call | tf_op jit(solution)/shard_map/joint/pallas_call | solution.py:576
  191.9 0.7 slice_reduce_fusion
  192.6 4.0 %fusion.6 = bf16[1,768,1024]{2,1,0:T(8,128)(2,1)} fusion(bf16[768,1024]{1,0:T(8,128)(2,1)} %bitcast.8, s32[768]{0:T(1024)S(1)} %slice_reduce_fusion, pred[768]{0:T(1024)(128)(4,1)S(1)} %broadcast_compare_fusion), kind=kOutput, calls=%fused_computation.4 | convolution fusion | flops 1209925632 | bytes 3149568 | tf_op jit(solution)/shard_map/dot_general | solution.py:651
  (2 shorter events, 0.0 us)
